TPU v7x, 32 devices: a whole 2x2x4 slice. The times are simulated.
32 devices in a mesh: site: 4 (over z), py: 2 (over x), px: 2 (over y), pz: 2 (over core).
Axes of the slice: x: 2, y: 2, z: 4, core: 2. Of those that a mesh axis runs over, the one named last changes fastest.
Arguments:
- initial_heat_state: float32 [32, 128, 64, 128], P(('site', 'py'), 'px', 'pz'), parts along dimension 0, may hold values from 0.2 to 1.8
- scaled_speed_north: float32 [32, 128, 64, 128], P(('site', 'py'), 'px', 'pz'), parts along dimension 0, may hold values from -0.3 to 0.3
- scaled_speed_east: float32 [32, 128, 64, 128], P(('site', 'py'), 'px', 'pz'), parts along dimension 0, may hold values from -0.3 to 0.3
- scaled_speed_upward: float32 [32, 128, 64, 128], P(('site', 'py'), 'px', 'pz'), parts along dimension 0, may hold values from -0.3 to 0.3
Outputs:
- temperature_end: float32 [32, 128, 64, 128], P(('site', 'py'), 'px', 'pz'), parts along dimension 0
There are 4 independent parts, one for each index of `site`. A program takes and returns all parts, laid end to end along the dimension named above; each array names one. Nothing has to cross between parts.
All inputs are finite; a program needn't handle non-finite values.
Results may differ from a plain program's by a relative error of at most 0.00002.
Values sent between devices are 32-bit elements; how exact they have to be, the bound alone decides.
A program may use at most 256 MiB of HBM per device.

v0:
```python
import jax
import jax.numpy as jnp
from jax import lax
from jax.sharding import PartitionSpec as P

STEPS = 4


def extended(cells, sides, width):
    for axis, dim in sides:
        count = lax.axis_size(axis)
        ends = count - 1
        head = lax.slice_in_dim(cells, 0, width, axis=dim)
        tail = lax.slice_in_dim(cells, cells.shape[dim] - width, cells.shape[dim], axis=dim)
        cells = jnp.concatenate(
            [
                lax.ppermute(tail, axis, [(i, (i + 1) % count) for i in range(ends)]),
                cells,
                lax.ppermute(head, axis, [((i + 1) % count, i) for i in range(ends)]),
            ],
            axis=dim,
        )
    return cells


def strip_edges(values, dims):
    for dim in dims:
        values = lax.slice_in_dim(values, 1, values.shape[dim] - 1, axis=dim)
    return values


def neighbour(values, dim, start, dims):
    others = [other for other in dims if other != dim]
    values = strip_edges(values, others)
    return lax.slice_in_dim(values, start, start + values.shape[dim] - 2, axis=dim)


def march_once(padded_with_frame, scaled_speed_north, scaled_speed_east, scaled_speed_upward):
    middle = strip_edges(padded_with_frame, (0, 1, 2))
    lower = [neighbour(padded_with_frame, dim, 0, (0, 1, 2)) for dim in (0, 1, 2)]
    upper = [neighbour(padded_with_frame, dim, 2, (0, 1, 2)) for dim in (0, 1, 2)]
    slopes = [above - below for above, below in zip(upper, lower)]
    smooth_rate = 0.05
    spread = lower[0] + upper[0] + lower[1] + upper[1] + lower[2] + upper[2] - 6.0 * middle
    return (
        middle
        - scaled_speed_north * slopes[0]
        - scaled_speed_east * slopes[1]
        - scaled_speed_upward * slopes[2]
        + smooth_rate * spread
    )


def body(initial_heat_state, scaled_speed_north, scaled_speed_east, scaled_speed_upward):
    for step in range(STEPS):
        padded_with_frame = extended(initial_heat_state, (("py", 0), ("px", 1), ("pz", 2)), 1)
        initial_heat_state = march_once(
            padded_with_frame, scaled_speed_north, scaled_speed_east, scaled_speed_upward
        )
    return initial_heat_state


def solution(mesh):
    in_specs = (
        P(("site", "py"), "px", "pz", None),
        P(("site", "py"), "px", "pz", None),
        P(("site", "py"), "px", "pz", None),
        P(("site", "py"), "px", "pz", None),
    )
    out_specs = P(("site", "py"), "px", "pz", None)
    return jax.shard_map(body, mesh=mesh, in_specs=in_specs, out_specs=out_specs, check_vma=False)
```

profile of v0, /device:TPU:0, one launch (start us, length us, event | category | flops | bytes accessed | tf_op | source)
XLA Modules:
  0.0 220.5 jit_solution(7663895514113652813)
XLA Ops:
  0.0 1.9 fusion.4
  1.9 5.1 %collective-permute-start.1 = (f32[1,64,32,128]{3,2,1,0:T(8,128)S(1)}, f32[1,64,32,128]{3,2,1,0:T(8,128)S(1)}, u32[]{:S(2)}, u32[]{:S(2)}) collective-permute-start(f32[1,64,32,128]{3,2,1,0:T(8,128)S(1)} %get-tuple-element.28), channel_id=1, source_target_pairs={{0,4},{1,5},{2,6},{3,7},{8,12},{9,13},{10,14},{11,15},{16,20},{17,... | collective-permute-start | bytes 3145736 | tf_op jit(solution)/shard_map/ppermute | solution.py:17
  8.3 21.0 %collective-permute-done.1 = f32[1,64,32,128]{3,2,1,0:T(8,128)S(1)} collective-permute-done((f32[1,64,32,128]{3,2,1,0:T(8,128)S(1)}, f32[1,64,32,128]{3,2,1,0:T(8,128)S(1)}, u32[]{:S(2)}, u32[]{:S(2)}) %collective-permute-start.1) | collective-permute-done | bytes 1048608 | tf_op jit(solution)/shard_map/ppermute | solution.py:17
  29.8 3.6 %collective-permute-done = f32[1,64,32,128]{3,2,1,0:T(8,128)S(1)} collective-permute-done((f32[1,64,32,128]{3,2,1,0:T(8,128)S(1)}, f32[1,64,32,128]{3,2,1,0:T(8,128)S(1)}, u32[]{:S(2)}, u32[]{:S(2)}) %collective-permute-start) | collective-permute-done | bytes 1048608 | tf_op jit(solution)/shard_map/ppermute | solution.py:19
  33.6 3.4 %collective-permute-start.3 = (f32[6,1,32,128]{3,2,1,0:T(8,128)S(1)}, f32[6,1,32,128]{3,2,1,0:T(8,128)S(1)}, u32[]{:S(2)}, u32[]{:S(2)}) collective-permute-start(f32[6,1,32,128]{3,2,1,0:T(8,128)S(1)} %get-tuple-element.19), channel_id=1, source_target_pairs={{0,2},{1,3},{4,6},{5,7},{8,10},{9,11},{12,14},{13,15},{16,18},{17,... | collective-permute-start | bytes 294920 | tf_op jit(solution)/shard_map/ppermute | solution.py:17
  39.2 4.3 %collective-permute-done.2 = f32[6,1,32,128]{3,2,1,0:T(8,128)S(1)} collective-permute-done((f32[6,1,32,128]{3,2,1,0:T(8,128)S(1)}, f32[6,1,32,128]{3,2,1,0:T(8,128)S(1)}, u32[]{:S(2)}, u32[]{:S(2)}) %collective-permute-start.2) | collective-permute-done | bytes 98336 | tf_op jit(solution)/shard_map/ppermute | solution.py:19
  45.2 3.1 %collective-permute-start.5 = (f32[6,66,1,128]{3,1,2,0:T(8,128)S(1)}, f32[6,66,1,128]{3,1,2,0:T(8,128)S(1)}, u32[]{:S(2)}, u32[]{:S(2)}) collective-permute-start(f32[6,66,1,128]{3,1,2,0:T(8,128)S(1)} %copy.27), channel_id=1, source_target_pairs={{0,1},{2,3},{4,5},{6,7},{8,9},{10,11},{12,13},{14,15},{16,17},{18,... | collective-permute-start | bytes 608264 | tf_op jit(solution)/shard_map/ppermute | solution.py:17
  49.5 16.7 %multiply_add_fusion.3 = f32[4,64,32,128]{3,2,1,0:T(8,128)S(1)} fusion(f32[4,64,32,128]{3,2,1,0:T(8,128)} %param.4, f32[4,64,32,128]{3,2,1,0:T(8,128)} %param.7, f32[6,66,1,128]{3,2,1,0:T(1,128)S(1)} %copy.26, f32[6,1,32,128]{3,2,1,0:T(8,128)} %copy-done.7, f32[6,64,32,128]{3,2,1,0:T(8,128)} %copy-done.4, f32[6,1,32,128]{3,2,1,0:T(8,128)} %copy-done.6, ...), kind=kLoop, calls=%fused_computation.67 | loop fusion | flops 29360128 | bytes 29962240 | tf_op jit(solution)/shard_map/add | solution.py:46
  69.2 21.7 %collective-permute-done.7 = f32[1,64,32,128]{3,2,1,0:T(8,128)S(1)} collective-permute-done((f32[1,64,32,128]{3,2,1,0:T(8,128)S(1)}, f32[1,64,32,128]{3,2,1,0:T(8,128)S(1)}, u32[]{:S(2)}, u32[]{:S(2)}) %collective-permute-start.7) | collective-permute-done | bytes 1048608 | tf_op jit(solution)/shard_map/ppermute | solution.py:17
  90.9 4.2 %collective-permute-done.6 = f32[1,64,32,128]{3,2,1,0:T(8,128)S(1)} collective-permute-done((f32[1,64,32,128]{3,2,1,0:T(8,128)S(1)}, f32[1,64,32,128]{3,2,1,0:T(8,128)S(1)}, u32[]{:S(2)}, u32[]{:S(2)}) %collective-permute-start.6) | collective-permute-done | bytes 1048608 | tf_op jit(solution)/shard_map/ppermute | solution.py:19
  95.1 1.9 collective-permute-start.9
  99.2 4.6 %collective-permute-done.8 = f32[6,1,32,128]{3,2,1,0:T(8,128)S(1)} collective-permute-done((f32[6,1,32,128]{3,2,1,0:T(8,128)S(1)}, f32[6,1,32,128]{3,2,1,0:T(8,128)S(1)}, u32[]{:S(2)}, u32[]{:S(2)}) %collective-permute-start.8) | collective-permute-done | bytes 98336 | tf_op jit(solution)/shard_map/ppermute | solution.py:19
  105.5 3.1 %collective-permute-start.11 = (f32[6,66,1,128]{3,1,2,0:T(8,128)S(1)}, f32[6,66,1,128]{3,1,2,0:T(8,128)S(1)}, u32[]{:S(2)}, u32[]{:S(2)}) collective-permute-start(f32[6,66,1,128]{3,1,2,0:T(8,128)S(1)} %copy.31), channel_id=1, source_target_pairs={{0,1},{2,3},{4,5},{6,7},{8,9},{10,11},{12,13},{14,15},{16,17},{18,... | collective-permute-start | bytes 608264 | tf_op jit(solution)/shard_map/ppermute | solution.py:17
  109.9 7.9 %multiply_add_fusion.2 = f32[4,64,32,128]{3,2,1,0:T(8,128)S(1)} fusion(f32[4,64,32,128]{3,2,1,0:T(8,128)S(1)} %multiply_add_fusion.3, f32[4,64,32,128]{3,2,1,0:T(8,128)S(1)} %copy-done, f32[6,66,1,128]{3,2,1,0:T(1,128)S(1)} %copy.30, f32[6,1,32,128]{3,2,1,0:T(8,128)S(1)} %collective-permute-done.8, f32[1,64,32,128]{3,2,1,0:T(8,128)S(1)} %collective-permute-done.6, ...), kind=kLoop, calls=%fused_computation.66 | loop fusion | flops 37748736 | bytes 23670784 | tf_op jit(solution)/shard_map/add | solution.py:46
  120.7 21.7 %collective-permute-done.13 = f32[1,64,32,128]{3,2,1,0:T(8,128)S(1)} collective-permute-done((f32[1,64,32,128]{3,2,1,0:T(8,128)S(1)}, f32[1,64,32,128]{3,2,1,0:T(8,128)S(1)}, u32[]{:S(2)}, u32[]{:S(2)}) %collective-permute-start.13) | collective-permute-done | bytes 1048608 | tf_op jit(solution)/shard_map/ppermute | solution.py:17
  142.4 4.2 %collective-permute-done.12 = f32[1,64,32,128]{3,2,1,0:T(8,128)S(1)} collective-permute-done((f32[1,64,32,128]{3,2,1,0:T(8,128)S(1)}, f32[1,64,32,128]{3,2,1,0:T(8,128)S(1)}, u32[]{:S(2)}, u32[]{:S(2)}) %collective-permute-start.12) | collective-permute-done | bytes 1048608 | tf_op jit(solution)/shard_map/ppermute | solution.py:19
  150.3 4.6 %collective-permute-done.14 = f32[6,1,32,128]{3,2,1,0:T(8,128)S(1)} collective-permute-done((f32[6,1,32,128]{3,2,1,0:T(8,128)S(1)}, f32[6,1,32,128]{3,2,1,0:T(8,128)S(1)}, u32[]{:S(2)}, u32[]{:S(2)}) %collective-permute-start.14) | collective-permute-done | bytes 98336 | tf_op jit(solution)/shard_map/ppermute | solution.py:19
  156.6 3.1 %collective-permute-start.17 = (f32[6,66,1,128]{3,1,2,0:T(8,128)S(1)}, f32[6,66,1,128]{3,1,2,0:T(8,128)S(1)}, u32[]{:S(2)}, u32[]{:S(2)}) collective-permute-start(f32[6,66,1,128]{3,1,2,0:T(8,128)S(1)} %copy.35), channel_id=1, source_target_pairs={{0,1},{2,3},{4,5},{6,7},{8,9},{10,11},{12,13},{14,15},{16,17},{18,... | collective-permute-start | bytes 608264 | tf_op jit(solution)/shard_map/ppermute | solution.py:17
  160.9 7.8 %multiply_add_fusion.1 = f32[4,64,32,128]{3,2,1,0:T(8,128)S(1)} fusion(f32[4,64,32,128]{3,2,1,0:T(8,128)S(1)} %multiply_add_fusion.2, f32[4,64,32,128]{3,2,1,0:T(8,128)S(1)} %copy-done, f32[6,66,1,128]{3,2,1,0:T(1,128)S(1)} %copy.34, f32[6,1,32,128]{3,2,1,0:T(8,128)S(1)} %collective-permute-done.14, f32[1,64,32,128]{3,2,1,0:T(8,128)S(1)} %collective-permute-done.12, ...), kind=kLoop, calls=%fused_computation.65 | loop fusion | flops 37748736 | bytes 23670784 | tf_op jit(solution)/shard_map/add | solution.py:46
  171.8 21.9 %collective-permute-done.19 = f32[1,64,32,128]{3,2,1,0:T(8,128)S(1)} collective-permute-done((f32[1,64,32,128]{3,2,1,0:T(8,128)S(1)}, f32[1,64,32,128]{3,2,1,0:T(8,128)S(1)}, u32[]{:S(2)}, u32[]{:S(2)}) %collective-permute-start.19) | collective-permute-done | bytes 1048608 | tf_op jit(solution)/shard_map/ppermute | solution.py:17
  193.6 4.2 %collective-permute-done.18 = f32[1,64,32,128]{3,2,1,0:T(8,128)S(1)} collective-permute-done((f32[1,64,32,128]{3,2,1,0:T(8,128)S(1)}, f32[1,64,32,128]{3,2,1,0:T(8,128)S(1)}, u32[]{:S(2)}, u32[]{:S(2)}) %collective-permute-start.18) | collective-permute-done | bytes 1048608 | tf_op jit(solution)/shard_map/ppermute | solution.py:19
  201.6 4.3 %collective-permute-done.20 = f32[6,1,32,128]{3,2,1,0:T(8,128)S(1)} collective-permute-done((f32[6,1,32,128]{3,2,1,0:T(8,128)S(1)}, f32[6,1,32,128]{3,2,1,0:T(8,128)S(1)}, u32[]{:S(2)}, u32[]{:S(2)}) %collective-permute-start.20) | collective-permute-done | bytes 98336 | tf_op jit(solution)/shard_map/ppermute | solution.py:19
  207.5 3.1 %collective-permute-start.23 = (f32[6,66,1,128]{3,1,2,0:T(8,128)S(1)}, f32[6,66,1,128]{3,1,2,0:T(8,128)S(1)}, u32[]{:S(2)}, u32[]{:S(2)}) collective-permute-start(f32[6,66,1,128]{3,1,2,0:T(8,128)S(1)} %copy.39), channel_id=1, source_target_pairs={{0,1},{2,3},{4,5},{6,7},{8,9},{10,11},{12,13},{14,15},{16,17},{18,... | collective-permute-start | bytes 608264 | tf_op jit(solution)/shard_map/ppermute | solution.py:17
  211.9 8.6 %multiply_add_fusion = f32[4,64,32,128]{3,2,1,0:T(8,128)} fusion(f32[4,64,32,128]{3,2,1,0:T(8,128)S(1)} %multiply_add_fusion.1, f32[4,64,32,128]{3,2,1,0:T(8,128)S(1)} %copy-done, f32[6,66,1,128]{3,2,1,0:T(1,128)S(1)} %copy.38, f32[6,1,32,128]{3,2,1,0:T(8,128)S(1)} %collective-permute-done.20, f32[1,64,32,128]{3,2,1,0:T(8,128)S(1)} %collective-permute-done.18, ...), kind=kLoop, calls=%fused_computation.64 | loop fusion | flops 37748736 | bytes 23670784 | tf_op jit(solution)/shard_map/add | solution.py:46
  (75 shorter events, 34.2 us)
Async XLA Ops:
  1.9 27.4 %collective-permute-start.1 = (f32[1,64,32,128]{3,2,1,0:T(8,128)S(1)}, f32[1,64,32,128]{3,2,1,0:T(8,128)S(1)}, u32[]{:S(2)}, u32[]{:S(2)}) collective-permute-start(f32[1,64,32,128]{3,2,1,0:T(8,128)S(1)} %get-tuple-element.28), channel_id=1, source_target_pairs={{0,4},{1,5},{2,6},{3,7},{8,12},{9,13},{10,14},{11,15},{16,20},{17,... | collective-permute-start | bytes 3145736 | tf_op jit(solution)/shard_map/ppermute | solution.py:17
  7.0 26.5 %collective-permute-start = (f32[1,64,32,128]{3,2,1,0:T(8,128)S(1)}, f32[1,64,32,128]{3,2,1,0:T(8,128)S(1)}, u32[]{:S(2)}, u32[]{:S(2)}) collective-permute-start(f32[1,64,32,128]{3,2,1,0:T(8,128)S(1)} %get-tuple-element.27), channel_id=1, source_target_pairs={{4,0},{5,1},{6,2},{7,3},{12,8},{13,9},{14,10},{15,11},{20,16},{21,... | collective-permute-start | bytes 3145736 | tf_op jit(solution)/shard_map/ppermute | solution.py:19
  33.6 5.6 %collective-permute-start.3 = (f32[6,1,32,128]{3,2,1,0:T(8,128)S(1)}, f32[6,1,32,128]{3,2,1,0:T(8,128)S(1)}, u32[]{:S(2)}, u32[]{:S(2)}) collective-permute-start(f32[6,1,32,128]{3,2,1,0:T(8,128)S(1)} %get-tuple-element.19), channel_id=1, source_target_pairs={{0,2},{1,3},{4,6},{5,7},{8,10},{9,11},{12,14},{13,15},{16,18},{17,... | collective-permute-start | bytes 294920 | tf_op jit(solution)/shard_map/ppermute | solution.py:17
  37.0 6.5 %collective-permute-start.2 = (f32[6,1,32,128]{3,2,1,0:T(8,128)S(1)}, f32[6,1,32,128]{3,2,1,0:T(8,128)S(1)}, u32[]{:S(2)}, u32[]{:S(2)}) collective-permute-start(f32[6,1,32,128]{3,2,1,0:T(8,128)S(1)} %get-tuple-element.20), channel_id=1, source_target_pairs={{2,0},{3,1},{6,4},{7,5},{10,8},{11,9},{14,12},{15,13},{18,16},{19,... | collective-permute-start | bytes 294920 | tf_op jit(solution)/shard_map/ppermute | solution.py:19
  43.8 4.4 %collective-permute-start.4 = (f32[6,66,1,128]{3,1,2,0:T(8,128)S(1)}, f32[6,66,1,128]{3,1,2,0:T(8,128)S(1)}, u32[]{:S(2)}, u32[]{:S(2)}) collective-permute-start(f32[6,66,1,128]{3,1,2,0:T(8,128)S(1)} %copy.25), channel_id=1, source_target_pairs={{1,0},{3,2},{5,4},{7,6},{9,8},{11,10},{13,12},{15,14},{17,16},{19,... | collective-permute-start | bytes 608264 | tf_op jit(solution)/shard_map/ppermute | solution.py:19
  45.2 4.1 %collective-permute-start.5 = (f32[6,66,1,128]{3,1,2,0:T(8,128)S(1)}, f32[6,66,1,128]{3,1,2,0:T(8,128)S(1)}, u32[]{:S(2)}, u32[]{:S(2)}) collective-permute-start(f32[6,66,1,128]{3,1,2,0:T(8,128)S(1)} %copy.27), channel_id=1, source_target_pairs={{0,1},{2,3},{4,5},{6,7},{8,9},{10,11},{12,13},{14,15},{16,17},{18,... | collective-permute-start | bytes 608264 | tf_op jit(solution)/shard_map/ppermute | solution.py:17
  66.4 24.5 %collective-permute-start.7 = (f32[1,64,32,128]{3,2,1,0:T(8,128)S(1)}, f32[1,64,32,128]{3,2,1,0:T(8,128)S(1)}, u32[]{:S(2)}, u32[]{:S(2)}) collective-permute-start(f32[1,64,32,128]{3,2,1,0:T(8,128)S(1)} %get-tuple-element.25), channel_id=1, source_target_pairs={{0,4},{1,5},{2,6},{3,7},{8,12},{9,13},{10,14},{11,15},{16,20},{17,... | collective-permute-start | bytes 3145736 | tf_op jit(solution)/shard_map/ppermute | solution.py:17
  67.9 27.2 %collective-permute-start.6 = (f32[1,64,32,128]{3,2,1,0:T(8,128)S(1)}, f32[1,64,32,128]{3,2,1,0:T(8,128)S(1)}, u32[]{:S(2)}, u32[]{:S(2)}) collective-permute-start(f32[1,64,32,128]{3,2,1,0:T(8,128)S(1)} %get-tuple-element.26), channel_id=1, source_target_pairs={{4,0},{5,1},{6,2},{7,3},{12,8},{13,9},{14,10},{15,11},{20,16},{21,... | collective-permute-start | bytes 3145736 | tf_op jit(solution)/shard_map/ppermute | solution.py:19
  95.1 4.1 %collective-permute-start.9 = (f32[6,1,32,128]{3,2,1,0:T(8,128)S(1)}, f32[6,1,32,128]{3,2,1,0:T(8,128)S(1)}, u32[]{:S(2)}, u32[]{:S(2)}) collective-permute-start(f32[6,1,32,128]{3,2,1,0:T(8,128)S(1)} %get-tuple-element.17), channel_id=1, source_target_pairs={{0,2},{1,3},{4,6},{5,7},{8,10},{9,11},{12,14},{13,15},{16,18},{17,... | collective-permute-start | bytes 294920 | tf_op jit(solution)/shard_map/ppermute | solution.py:17
  97.1 6.8 %collective-permute-start.8 = (f32[6,1,32,128]{3,2,1,0:T(8,128)S(1)}, f32[6,1,32,128]{3,2,1,0:T(8,128)S(1)}, u32[]{:S(2)}, u32[]{:S(2)}) collective-permute-start(f32[6,1,32,128]{3,2,1,0:T(8,128)S(1)} %get-tuple-element.18), channel_id=1, source_target_pairs={{2,0},{3,1},{6,4},{7,5},{10,8},{11,9},{14,12},{15,13},{18,16},{19,... | collective-permute-start | bytes 294920 | tf_op jit(solution)/shard_map/ppermute | solution.py:19
  104.2 4.4 %collective-permute-start.10 = (f32[6,66,1,128]{3,1,2,0:T(8,128)S(1)}, f32[6,66,1,128]{3,1,2,0:T(8,128)S(1)}, u32[]{:S(2)}, u32[]{:S(2)}) collective-permute-start(f32[6,66,1,128]{3,1,2,0:T(8,128)S(1)} %copy.29), channel_id=1, source_target_pairs={{1,0},{3,2},{5,4},{7,6},{9,8},{11,10},{13,12},{15,14},{17,16},{19,... | collective-permute-start | bytes 608264 | tf_op jit(solution)/shard_map/ppermute | solution.py:19
  105.5 4.1 %collective-permute-start.11 = (f32[6,66,1,128]{3,1,2,0:T(8,128)S(1)}, f32[6,66,1,128]{3,1,2,0:T(8,128)S(1)}, u32[]{:S(2)}, u32[]{:S(2)}) collective-permute-start(f32[6,66,1,128]{3,1,2,0:T(8,128)S(1)} %copy.31), channel_id=1, source_target_pairs={{0,1},{2,3},{4,5},{6,7},{8,9},{10,11},{12,13},{14,15},{16,17},{18,... | collective-permute-start | bytes 608264 | tf_op jit(solution)/shard_map/ppermute | solution.py:17
  117.9 24.5 %collective-permute-start.13 = (f32[1,64,32,128]{3,2,1,0:T(8,128)S(1)}, f32[1,64,32,128]{3,2,1,0:T(8,128)S(1)}, u32[]{:S(2)}, u32[]{:S(2)}) collective-permute-start(f32[1,64,32,128]{3,2,1,0:T(8,128)S(1)} %get-tuple-element.23), channel_id=1, source_target_pairs={{0,4},{1,5},{2,6},{3,7},{8,12},{9,13},{10,14},{11,15},{16,20},{17,... | collective-permute-start | bytes 3145736 | tf_op jit(solution)/shard_map/ppermute | solution.py:17
  119.4 27.2 %collective-permute-start.12 = (f32[1,64,32,128]{3,2,1,0:T(8,128)S(1)}, f32[1,64,32,128]{3,2,1,0:T(8,128)S(1)}, u32[]{:S(2)}, u32[]{:S(2)}) collective-permute-start(f32[1,64,32,128]{3,2,1,0:T(8,128)S(1)} %get-tuple-element.24), channel_id=1, source_target_pairs={{4,0},{5,1},{6,2},{7,3},{12,8},{13,9},{14,10},{15,11},{20,16},{21,... | collective-permute-start | bytes 3145736 | tf_op jit(solution)/shard_map/ppermute | solution.py:19
  146.6 3.7 %collective-permute-start.15 = (f32[6,1,32,128]{3,2,1,0:T(8,128)S(1)}, f32[6,1,32,128]{3,2,1,0:T(8,128)S(1)}, u32[]{:S(2)}, u32[]{:S(2)}) collective-permute-start(f32[6,1,32,128]{3,2,1,0:T(8,128)S(1)} %get-tuple-element.15), channel_id=1, source_target_pairs={{0,2},{1,3},{4,6},{5,7},{8,10},{9,11},{12,14},{13,15},{16,18},{17,... | collective-permute-start | bytes 294920 | tf_op jit(solution)/shard_map/ppermute | solution.py:17
  148.2 6.8 %collective-permute-start.14 = (f32[6,1,32,128]{3,2,1,0:T(8,128)S(1)}, f32[6,1,32,128]{3,2,1,0:T(8,128)S(1)}, u32[]{:S(2)}, u32[]{:S(2)}) collective-permute-start(f32[6,1,32,128]{3,2,1,0:T(8,128)S(1)} %get-tuple-element.16), channel_id=1, source_target_pairs={{2,0},{3,1},{6,4},{7,5},{10,8},{11,9},{14,12},{15,13},{18,16},{19,... | collective-permute-start | bytes 294920 | tf_op jit(solution)/shard_map/ppermute | solution.py:19
  155.3 4.4 %collective-permute-start.16 = (f32[6,66,1,128]{3,1,2,0:T(8,128)S(1)}, f32[6,66,1,128]{3,1,2,0:T(8,128)S(1)}, u32[]{:S(2)}, u32[]{:S(2)}) collective-permute-start(f32[6,66,1,128]{3,1,2,0:T(8,128)S(1)} %copy.33), channel_id=1, source_target_pairs={{1,0},{3,2},{5,4},{7,6},{9,8},{11,10},{13,12},{15,14},{17,16},{19,... | collective-permute-start | bytes 608264 | tf_op jit(solution)/shard_map/ppermute | solution.py:19
  156.6 4.1 %collective-permute-start.17 = (f32[6,66,1,128]{3,1,2,0:T(8,128)S(1)}, f32[6,66,1,128]{3,1,2,0:T(8,128)S(1)}, u32[]{:S(2)}, u32[]{:S(2)}) collective-permute-start(f32[6,66,1,128]{3,1,2,0:T(8,128)S(1)} %copy.35), channel_id=1, source_target_pairs={{0,1},{2,3},{4,5},{6,7},{8,9},{10,11},{12,13},{14,15},{16,17},{18,... | collective-permute-start | bytes 608264 | tf_op jit(solution)/shard_map/ppermute | solution.py:17
  168.9 24.7 %collective-permute-start.19 = (f32[1,64,32,128]{3,2,1,0:T(8,128)S(1)}, f32[1,64,32,128]{3,2,1,0:T(8,128)S(1)}, u32[]{:S(2)}, u32[]{:S(2)}) collective-permute-start(f32[1,64,32,128]{3,2,1,0:T(8,128)S(1)} %get-tuple-element.21), channel_id=1, source_target_pairs={{0,4},{1,5},{2,6},{3,7},{8,12},{9,13},{10,14},{11,15},{16,20},{17,... | collective-permute-start | bytes 3145736 | tf_op jit(solution)/shard_map/ppermute | solution.py:17
  170.5 27.3 %collective-permute-start.18 = (f32[1,64,32,128]{3,2,1,0:T(8,128)S(1)}, f32[1,64,32,128]{3,2,1,0:T(8,128)S(1)}, u32[]{:S(2)}, u32[]{:S(2)}) collective-permute-start(f32[1,64,32,128]{3,2,1,0:T(8,128)S(1)} %get-tuple-element.22), channel_id=1, source_target_pairs={{4,0},{5,1},{6,2},{7,3},{12,8},{13,9},{14,10},{15,11},{20,16},{21,... | collective-permute-start | bytes 3145736 | tf_op jit(solution)/shard_map/ppermute | solution.py:19
  197.8 3.7 %collective-permute-start.21 = (f32[6,1,32,128]{3,2,1,0:T(8,128)S(1)}, f32[6,1,32,128]{3,2,1,0:T(8,128)S(1)}, u32[]{:S(2)}, u32[]{:S(2)}) collective-permute-start(f32[6,1,32,128]{3,2,1,0:T(8,128)S(1)} %get-tuple-element.13), channel_id=1, source_target_pairs={{0,2},{1,3},{4,6},{5,7},{8,10},{9,11},{12,14},{13,15},{16,18},{17,... | collective-permute-start | bytes 294920 | tf_op jit(solution)/shard_map/ppermute | solution.py:17
  199.4 6.5 %collective-permute-start.20 = (f32[6,1,32,128]{3,2,1,0:T(8,128)S(1)}, f32[6,1,32,128]{3,2,1,0:T(8,128)S(1)}, u32[]{:S(2)}, u32[]{:S(2)}) collective-permute-start(f32[6,1,32,128]{3,2,1,0:T(8,128)S(1)} %get-tuple-element.14), channel_id=1, source_target_pairs={{2,0},{3,1},{6,4},{7,5},{10,8},{11,9},{14,12},{15,13},{18,16},{19,... | collective-permute-start | bytes 294920 | tf_op jit(solution)/shard_map/ppermute | solution.py:19
  206.2 4.4 %collective-permute-start.22 = (f32[6,66,1,128]{3,1,2,0:T(8,128)S(1)}, f32[6,66,1,128]{3,1,2,0:T(8,128)S(1)}, u32[]{:S(2)}, u32[]{:S(2)}) collective-permute-start(f32[6,66,1,128]{3,1,2,0:T(8,128)S(1)} %copy.37), channel_id=1, source_target_pairs={{1,0},{3,2},{5,4},{7,6},{9,8},{11,10},{13,12},{15,14},{17,16},{19,... | collective-permute-start | bytes 608264 | tf_op jit(solution)/shard_map/ppermute | solution.py:19
  207.5 4.1 %collective-permute-start.23 = (f32[6,66,1,128]{3,1,2,0:T(8,128)S(1)}, f32[6,66,1,128]{3,1,2,0:T(8,128)S(1)}, u32[]{:S(2)}, u32[]{:S(2)}) collective-permute-start(f32[6,66,1,128]{3,1,2,0:T(8,128)S(1)} %copy.39), channel_id=1, source_target_pairs={{0,1},{2,3},{4,5},{6,7},{8,9},{10,11},{12,13},{14,15},{16,17},{18,... | collective-permute-start | bytes 608264 | tf_op jit(solution)/shard_map/ppermute | solution.py:17
  (8 other events, 114.1 us)
where the time goes:
time: 221 us; the launch traced here: 220 us
  waiting for transfers between devices  127 us (57%)
  starting transfers between devices  46.3 us (21%)
  other arithmetic  42.1 us (19%)
  local copies, waits for them, and re-layouts  4.82 us (2%)
    ppermute x12, waiting for transfers between devices, extended(): lax.ppermute(tail, axis, [(i, (i + 1) % count) for i in range(ends)])  92.7 us
    add x4, other arithmetic, march_once(): middle - scaled_speed_north * slopes[0] - scaled_speed_east * slopes[1]  41 us
    ppermute x12, waiting for transfers between devices, extended(): lax.ppermute(head, axis, [((i + 1) % count, i) for i in range(ends)])  34 us
    ppermute x12, starting transfers between devices, extended(): lax.ppermute(tail, axis, [(i, (i + 1) % count) for i in range(ends)])  30.3 us
    ppermute x12, starting transfers between devices, extended(): lax.ppermute(head, axis, [((i + 1) % count, i) for i in range(ends)])  16 us
  transfers between devices with their start and end apart: 24, of which 20 were waited for; matrix products, arithmetic and copies ran while one was open for 1% of the time, Pallas kernels for 0%

commit v1 on v0

v1 whole, which is shorter than its diff:
```python
import functools

import jax
import jax.numpy as jnp
from jax import lax
from jax.experimental import pallas as pl
from jax.experimental.pallas import tpu as pltpu
from jax.sharding import PartitionSpec as P

STEPS = 4
PAD = 8
MESH = pl.DeviceIdType.MESH


def kernel(
    counts, chunks, x, vn, ve, vu, out, s, w,
    load_sem, speed_sem, out_sem,
    py_send, py_recv, px_send, px_recv, pz_send, pz_recv,
):
    planes, rows, depth, _ = x.shape
    span = rows // chunks
    cells = pl.ds(PAD, depth)
    speeds = (vn, ve, vu)
    axes = ("py", "px", "pz")
    index = {axis: lax.axis_index(axis) for axis in axes}

    def sends(axis, way):
        return index[axis] < counts[axis] - 1 if way == 0 else index[axis] > 0

    def receives(axis, way):
        return sends(axis, 1 - way)

    def target(axis, way):
        count = counts[axis]
        return {axis: lax.rem(index[axis] + (1 if way == 0 else count - 1), count)}

    def chunk_of(j):
        half = j // 2
        return half + (j % 2) * (chunks - 1 - 2 * half)

    def remote(src, dst, send, recv, axis, way):
        return pltpu.make_async_remote_copy(
            src_ref=src, dst_ref=dst, send_sem=send, recv_sem=recv,
            device_id=target(axis, way), device_id_type=MESH,
        )

    def py_copy(way, t, c):
        plane = planes if way == 0 else 1
        here = pl.ds(1 + c * span, span)
        src = x.at[plane - 1, pl.ds(c * span, span)] if t == 0 else s.at[t, plane, here, cells]
        dst = s.at[t, 0 if way == 0 else planes + 1, here, cells]
        return remote(src, dst, py_send.at[way, t, c], py_recv.at[way, t, c], "py", way)

    def px_copy(way, t):
        row = rows if way == 0 else 1
        inner = pl.ds(1, planes)
        src = x.at[:, row - 1] if t == 0 else s.at[t, inner, row, cells]
        dst = s.at[t, inner, 0 if way == 0 else rows + 1, cells]
        return remote(src, dst, px_send.at[way, t], px_recv.at[way, t], "px", way)

    def pz_copy(way, t, c):
        inner, here = pl.ds(1, planes), pl.ds(1 + c * span, span)
        first = depth - PAD if way == 0 else 0
        if t == 0:
            src = x.at[:, pl.ds(c * span, span), pl.ds(first, PAD)]
        else:
            src = s.at[t, inner, here, pl.ds(PAD + first, PAD)]
        dst = s.at[t, inner, here, pl.ds(0 if way == 0 else PAD + depth, PAD)]
        return remote(src, dst, pz_send.at[way, t, c], pz_recv.at[way, t, c], "pz", way)

    def each(axis, test, action):
        if counts[axis] > 1:
            for way in (0, 1):
                pl.when(test(axis, way))(functools.partial(action, way))

    def send_edges(t, j, c):
        each("py", sends, lambda way: py_copy(way, t, c).start())
        each("pz", sends, lambda way: pz_copy(way, t, c).start())
        if counts["px"] > 1:
            pl.when((j == 0) & sends("px", 1))(lambda: px_copy(1, t).start())
            pl.when((j == 1) & sends("px", 0))(lambda: px_copy(0, t).start())

    def wait_edges(t, j, c):
        each("py", receives, lambda way: py_copy(way, t, c).wait_recv())
        each("pz", receives, lambda way: pz_copy(way, t, c).wait_recv())
        if counts["px"] > 1:
            pl.when((j == 0) & receives("px", 0))(lambda: px_copy(0, t).wait_recv())
            pl.when((j == 1) & receives("px", 1))(lambda: px_copy(1, t).wait_recv())

    def speed_copy(k, c):
        here = pl.ds(c * span, span)
        return pltpu.make_async_copy(speeds[k].at[:, here], w.at[k, :, here], speed_sem.at[k, c])

    def out_copy(c):
        return pltpu.make_async_copy(
            s.at[0, pl.ds(1, planes), pl.ds(1 + c * span, span), cells],
            out.at[:, pl.ds(c * span, span)],
            out_sem.at[c],
        )

    def over_chunks(action):
        lax.fori_loop(0, chunks, lambda j, _: (action(j, chunk_of(j)), None)[1], None)

    load = pltpu.make_async_copy(
        x, s.at[0, pl.ds(1, planes), pl.ds(1, rows), cells], load_sem
    )
    load.start()

    barrier = pltpu.get_barrier_semaphore()
    greeted = 0
    for axis in axes:
        each(axis, sends, lambda way, axis=axis: pl.semaphore_signal(
            barrier, inc=1, device_id=target(axis, way), device_id_type=MESH))
        if counts[axis] > 1:
            for way in (0, 1):
                greeted = greeted + sends(axis, way).astype(jnp.int32)
    pl.semaphore_wait(barrier, greeted)

    over_chunks(lambda j, c: send_edges(0, j, c))
    over_chunks(lambda j, c: [speed_copy(k, c).start() for k in range(3)])

    def clear(axis, way):
        lanes = s.shape[-1]

        def fill(t, _):
            if axis == "py":
                plane = 0 if way == 0 else planes + 1

                def row_fill(r, _):
                    s[t, plane, 1 + r, PAD:PAD + depth, :] = jnp.zeros((depth, lanes), s.dtype)
                    return None

                lax.fori_loop(0, rows, row_fill, None)
            elif axis == "px":
                row = 0 if way == 0 else rows + 1
                for p in range(1, planes + 1):
                    s[t, p, row, PAD:PAD + depth, :] = jnp.zeros((depth, lanes), s.dtype)
            else:
                first = 0 if way == 0 else PAD + depth

                def row_fill(r, _):
                    for p in range(1, planes + 1):
                        s[t, p, 1 + r, first:first + PAD, :] = jnp.zeros((PAD, lanes), s.dtype)
                    return None

                lax.fori_loop(0, rows, row_fill, None)
            return None

        lax.fori_loop(0, STEPS, fill, None)

    for axis in axes:
        for way in (0, 1):
            pl.when(jnp.logical_not(receives(axis, way)))(functools.partial(clear, axis, way))

    load.wait()

    for t in range(STEPS):
        last = t == STEPS - 1
        into = 0 if last else t + 1

        def march(j, c, t=t, last=last, into=into):
            if t == 0:
                for k in range(3):
                    speed_copy(k, c).wait()
            wait_edges(t, j, c)

            def row(i, _):
                r = c * span + i
                for z in range(PAD, PAD + depth, 8):
                    here = slice(z, z + 8)
                    column = [s[t, p, r + 1, here, :] for p in range(planes + 2)]
                    for p in range(planes):
                        lower = (column[p], s[t, p + 1, r, here, :], s[t, p + 1, r + 1, z - 1:z + 7, :])
                        upper = (column[p + 2], s[t, p + 1, r + 2, here, :], s[t, p + 1, r + 1, z + 1:z + 9, :])
                        middle = column[p + 1]
                        value = middle
                        for k in range(3):
                            value = value - w[k, p, r, z - PAD:z - PAD + 8, :] * (upper[k] - lower[k])
                        spread = (lower[0] + upper[0]) + (lower[1] + upper[1]) + (lower[2] + upper[2])
                        s[into, p + 1, r + 1, here, :] = value + 0.05 * (spread - 6.0 * middle)
                return None

            lax.fori_loop(0, span, row, None)
            if last:
                out_copy(c).start()
            else:
                send_edges(t + 1, j, c)

        over_chunks(march)

    for t in range(STEPS):
        over_chunks(lambda j, c, t=t: [
            each("py", sends, lambda way: py_copy(way, t, c).wait_send()),
            each("pz", sends, lambda way: pz_copy(way, t, c).wait_send()),
        ])
        each("px", sends, lambda way, t=t: px_copy(way, t).wait_send())
    over_chunks(lambda j, c: out_copy(c).wait())


def body(counts, x, vn, ve, vu):
    planes, rows, depth, lanes = x.shape
    chunks = 8
    dma = pltpu.SemaphoreType.DMA
    return pl.pallas_call(
        functools.partial(kernel, counts, chunks),
        out_shape=jax.ShapeDtypeStruct(x.shape, x.dtype),
        in_specs=[pl.BlockSpec(memory_space=pl.ANY)] * 4,
        out_specs=pl.BlockSpec(memory_space=pl.ANY),
        scratch_shapes=[
            pltpu.VMEM((STEPS, planes + 2, rows + 2, depth + 2 * PAD, lanes), x.dtype),
            pltpu.VMEM((3, planes, rows, depth, lanes), x.dtype),
            dma(()),
            dma((3, chunks)),
            dma((chunks,)),
            dma((2, STEPS, chunks)),
            dma((2, STEPS, chunks)),
            dma((2, STEPS)),
            dma((2, STEPS)),
            dma((2, STEPS, chunks)),
            dma((2, STEPS, chunks)),
        ],
        compiler_params=pltpu.CompilerParams(
            collective_id=0, has_side_effects=True, vmem_limit_bytes=67043328
        ),
    )(x, vn, ve, vu)


def solution(mesh):
    counts = {axis: mesh.shape[axis] for axis in ("py", "px", "pz")}
    spec = P(("site", "py"), "px", "pz", None)
    return jax.shard_map(
        functools.partial(body, counts), mesh=mesh, in_specs=(spec,) * 4, out_specs=spec,
        check_vma=False,
    )
```

time: 221 us -> 104 us (0.47)
  waiting for transfers between devices: 127 us -> 0 us
  Pallas kernels: 0 us -> 98.9 us
  starting transfers between devices: 46.3 us -> 0 us
  other arithmetic: 42.1 us -> 0 us
    ppermute x24 -> x0, waiting for transfers between devices: 127 us -> none  [the longest x12 92.7 us: extended(): lax.ppermute(tail, axis, [(i, (i + 1) % count) for i in range(ends)])]
    pallas_call x0 -> x1, Pallas kernels: none -> 98.9 us  [body(): pl.pallas_call(functools.partial(kernel, counts, chunks), out_shape=jax.S...]
    ppermute x24 -> x0, starting transfers between devices: 46.3 us -> none  [the longest x12 30.3 us: extended(): lax.ppermute(tail, axis, [(i, (i + 1) % count) for i in range(ends)])]
    add x4 -> x0, other arithmetic: 41 us -> none  [march_once(): middle - scaled_speed_north * slopes[0] - scaled_speed_east * slopes[1]]
    unnamed x18 -> x1, local copies, waits for them, and re-layouts: 0.55 us -> 4.64 us
    slice x13 -> x0, local copies, waits for them, and re-layouts: 2.53 us -> none  [the longest x5 1.93 us: extended(): head = lax.slice_in_dim(cells, 0, width, axis=dim)]
  transfers between devices with their start and end apart: 24 -> 0, of which waited for: 20 -> 0; matrix products, arithmetic and copies ran while one was open for 1% -> 0% of each run, Pallas kernels for 0% -> 0%
where the time goes in v1:
time: 104 us
  Pallas kernels  98.9 us (95%)
  local copies, waits for them, and re-layouts  4.64 us (4%)
    pallas_call x1, Pallas kernels, body(): pl.pallas_call(functools.partial(kernel, counts, chunks), out_shape=jax.S...  98.9 us
    unnamed x1, local copies, waits for them, and re-layouts  4.64 us

profile of v1, /device:TPU:0, one launch (start us, length us, event | category | flops | bytes accessed | tf_op | source)
XLA Modules:
  0.0 103.5 jit_solution(15749347919231194240)
XLA Ops:
  0.0 98.9 %shard_map.46 = f32[4,64,32,128]{3,2,1,0:T(8,128)} custom-call(f32[4,64,32,128]{3,2,1,0:T(8,128)} %x.1, f32[4,64,32,128]{3,2,1,0:T(8,128)} %vn.1, f32[4,64,32,128]{3,2,1,0:T(8,128)} %ve.1, f32[4,64,32,128]{3,2,1,0:T(8,128)} %vu.1), custom_call_target="tpu_custom_call" | custom-call | tf_op jit(solution)/shard_map/pallas_call | solution.py:204
  98.9 4.6 %copy.6 = f32[4,64,32,128]{3,2,1,0:T(8,128)} copy(f32[4,64,32,128]{3,2,1,0:T(8,128)} %shard_map.46) | data formatting | bytes 8388608

commit v2 on v1

v2 whole, which is shorter than its diff:
```python
import functools

import jax
import jax.numpy as jnp
from jax import lax
from jax.experimental import pallas as pl
from jax.experimental.pallas import tpu as pltpu
from jax.sharding import PartitionSpec as P

STEPS = 4
CHUNKS = 16
PAD = 8
MESH = pl.DeviceIdType.MESH


def kernel(
    counts, chunks, x, vn, ve, vu, out, s, w,
    edge_sem, load_sem, speed_sem,
    py_send, py_recv, px_send, px_recv, pz_send, pz_recv,
):
    planes, rows, depth, _ = x.shape
    span = rows // chunks
    cells = pl.ds(PAD, depth)
    speeds = (vn, ve, vu)
    outer = sorted({1, planes})
    inner_count = planes - 2
    axes = ("py", "px", "pz")
    index = {axis: lax.axis_index(axis) for axis in axes}

    def sends(axis, way):
        return index[axis] < counts[axis] - 1 if way == 0 else index[axis] > 0

    def receives(axis, way):
        return sends(axis, 1 - way)

    def target(axis, way):
        count = counts[axis]
        return {axis: lax.rem(index[axis] + (1 if way == 0 else count - 1), count)}

    def chunk_of(j):
        half = j // 2
        return half + (j % 2) * (chunks - 1 - 2 * half)

    def remote(src, dst, send, recv, axis, way):
        return pltpu.make_async_remote_copy(
            src_ref=src, dst_ref=dst, send_sem=send, recv_sem=recv,
            device_id=target(axis, way), device_id_type=MESH,
        )

    def py_copy(way, t, c):
        plane = planes if way == 0 else 1
        here = pl.ds(1 + c * span, span)
        src = s.at[t, plane, here, cells]
        dst = s.at[t, 0 if way == 0 else planes + 1, here, cells]
        return remote(src, dst, py_send.at[way, t], py_recv.at[way, t, c], "py", way)

    def px_copy(way, t):
        row = rows if way == 0 else 1
        inner = pl.ds(1, planes)
        src = x.at[:, row - 1] if t == 0 else s.at[t, inner, row, cells]
        dst = s.at[t, inner, 0 if way == 0 else rows + 1, cells]
        return remote(src, dst, px_send.at[way, t], px_recv.at[way, t], "px", way)

    def pz_copy(way, t, c):
        inner, here = pl.ds(1, planes), pl.ds(1 + c * span, span)
        first = depth - PAD if way == 0 else 0
        if t == 0:
            src = x.at[:, pl.ds(c * span, span), pl.ds(first, PAD)]
        else:
            src = s.at[t, inner, here, pl.ds(PAD + first, PAD)]
        dst = s.at[t, inner, here, pl.ds(0 if way == 0 else PAD + depth, PAD)]
        return remote(src, dst, pz_send.at[way, t], pz_recv.at[way, t, c], "pz", way)

    def wait_sent(t):
        inner, here = pl.ds(1, planes), pl.ds(1, rows)

        def py_wait(way):
            block = s.at[t, planes if way == 0 else 1, here, cells]
            remote(block, block, py_send.at[way, t], py_recv.at[way, t, 0], "py", way).wait_send()

        def pz_wait(way):
            block = s.at[t, inner, here, pl.ds(PAD, PAD)]
            remote(block, block, pz_send.at[way, t], pz_recv.at[way, t, 0], "pz", way).wait_send()

        each("py", sends, py_wait)
        each("pz", sends, pz_wait)
        each("px", sends, lambda way: px_copy(way, t).wait_send())

    def each(axis, test, action):
        if counts[axis] > 1:
            for way in (0, 1):
                pl.when(test(axis, way))(functools.partial(action, way))

    def send_py(t, c):
        each("py", sends, lambda way: py_copy(way, t, c).start())

    def send_rest(t, c):
        each("pz", sends, lambda way: pz_copy(way, t, c).start())
        if counts["px"] > 1:
            pl.when((c == 0) & sends("px", 1))(lambda: px_copy(1, t).start())
            pl.when((c == chunks - 1) & sends("px", 0))(lambda: px_copy(0, t).start())

    def wait_py(t, c):
        each("py", receives, lambda way: py_copy(way, t, c).wait_recv())

    def wait_rest(t, c):
        each("pz", receives, lambda way: pz_copy(way, t, c).wait_recv())
        if counts["px"] > 1:
            pl.when((c == 0) & receives("px", 0))(lambda: px_copy(0, t).wait_recv())
            pl.when((c == chunks - 1) & receives("px", 1))(lambda: px_copy(1, t).wait_recv())

    def speed_copy(k, c):
        here = pl.ds(c * span, span)
        return pltpu.make_async_copy(speeds[k].at[:, here], w.at[k, :, here], speed_sem.at[c])

    def wait_speeds(c):
        block = w.at[:, :, pl.ds(c * span, span)]
        pltpu.make_async_copy(block, block, speed_sem.at[c]).wait()

    def edge_load(k, c):
        return pltpu.make_async_copy(
            x.at[outer[k] - 1, pl.ds(c * span, span)],
            s.at[0, outer[k], pl.ds(1 + c * span, span), cells],
            edge_sem.at[k, c],
        )

    def over_chunks(action):
        lax.fori_loop(0, chunks, lambda j, _: (action(j, chunk_of(j)), None)[1], None)

    over_chunks(lambda j, c: [edge_load(k, c).start() for k in range(len(outer))])
    if inner_count > 0:
        load = pltpu.make_async_copy(
            x.at[pl.ds(1, inner_count)],
            s.at[0, pl.ds(2, inner_count), pl.ds(1, rows), cells],
            load_sem,
        )
        load.start()

    barrier = pltpu.get_barrier_semaphore()
    greeted = 0
    for axis in axes:
        each(axis, sends, lambda way, axis=axis: pl.semaphore_signal(
            barrier, inc=1, device_id=target(axis, way), device_id_type=MESH))
        if counts[axis] > 1:
            for way in (0, 1):
                greeted = greeted + sends(axis, way).astype(jnp.int32)
    pl.semaphore_wait(barrier, greeted)

    def first(j, c):
        for k in range(len(outer)):
            edge_load(k, c).wait()
        send_py(0, c)

    over_chunks(first)
    over_chunks(lambda j, c: send_rest(0, c))
    over_chunks(lambda j, c: [speed_copy(k, c).start() for k in range(3)])

    def clear(axis, way):
        lanes = s.shape[-1]

        def fill(t, _):
            if axis == "py":
                plane = 0 if way == 0 else planes + 1

                def row_fill(r, _):
                    s[t, plane, 1 + r, PAD:PAD + depth, :] = jnp.zeros((depth, lanes), s.dtype)
                    return None

                lax.fori_loop(0, rows, row_fill, None)
            elif axis == "px":
                row = 0 if way == 0 else rows + 1
                for p in range(1, planes + 1):
                    s[t, p, row, PAD:PAD + depth, :] = jnp.zeros((depth, lanes), s.dtype)
            else:
                first = 0 if way == 0 else PAD + depth

                def row_fill(r, _):
                    for p in range(1, planes + 1):
                        s[t, p, 1 + r, first:first + PAD, :] = jnp.zeros((PAD, lanes), s.dtype)
                    return None

                lax.fori_loop(0, rows, row_fill, None)
            return None

        lax.fori_loop(0, STEPS, fill, None)

    for axis in axes:
        for way in (0, 1):
            pl.when(jnp.logical_not(receives(axis, way)))(functools.partial(clear, axis, way))

    if inner_count > 0:
        load.wait()

    def update(t, c, wanted):
        def row(i, _):
            r = c * span + i
            for z in range(PAD, PAD + depth, 8):
                here = slice(z, z + 8)
                column = {}
                for p in wanted:
                    for q in (p, p + 1, p + 2):
                        if q not in column:
                            column[q] = s[t, q, r + 1, here, :]
                    lower = (column[p], s[t, p + 1, r, here, :], s[t, p + 1, r + 1, z - 1:z + 7, :])
                    upper = (column[p + 2], s[t, p + 1, r + 2, here, :], s[t, p + 1, r + 1, z + 1:z + 9, :])
                    middle = column[p + 1]
                    value = middle
                    for k in range(3):
                        value = value - w[k, p, r, z - PAD:z - PAD + 8, :] * (upper[k] - lower[k])
                    spread = (lower[0] + upper[0]) + (lower[1] + upper[1]) + (lower[2] + upper[2])
                    value = value + 0.05 * (spread - 6.0 * middle)
                    if t == STEPS - 1:
                        out[p, r, z - PAD:z - PAD + 8, :] = value
                    else:
                        s[t + 1, p + 1, r + 1, here, :] = value
            return None

        lax.fori_loop(0, span, row, None)

    for t in range(STEPS - 1):
        def march(j, c, t=t):
            if t == 0:
                wait_speeds(c)
            wait_py(t, c)
            wait_rest(t, c)
            update(t, c, range(planes))
            send_py(t + 1, c)
            send_rest(t + 1, c)

        over_chunks(march)

    def march_inner(j, c):
        wait_rest(STEPS - 1, c)
        update(STEPS - 1, c, range(1, planes - 1))

    def march_outer(j, c):
        wait_py(STEPS - 1, c)
        update(STEPS - 1, c, [p - 1 for p in outer])

    over_chunks(march_inner)
    for t in range(STEPS - 1):
        wait_sent(t)
    over_chunks(march_outer)
    wait_sent(STEPS - 1)


def body(counts, x, vn, ve, vu):
    planes, rows, depth, lanes = x.shape
    chunks = max(n for n in (CHUNKS, 8, 1) if rows % n == 0)
    dma = pltpu.SemaphoreType.DMA
    return pl.pallas_call(
        functools.partial(kernel, counts, chunks),
        out_shape=pltpu.VMEM(x.shape, x.dtype),
        in_specs=[pl.BlockSpec(memory_space=pl.ANY)] * 4,
        out_specs=pl.BlockSpec(memory_space=pltpu.VMEM),
        scratch_shapes=[
            pltpu.VMEM((STEPS, planes + 2, rows + 2, depth + 2 * PAD, lanes), x.dtype),
            pltpu.VMEM((3, planes, rows, depth, lanes), x.dtype),
            dma((2, chunks)),
            dma(()),
            dma((chunks,)),
            dma((2, STEPS)),
            dma((2, STEPS, chunks)),
            dma((2, STEPS)),
            dma((2, STEPS)),
            dma((2, STEPS)),
            dma((2, STEPS, chunks)),
        ],
        compiler_params=pltpu.CompilerParams(
            collective_id=0, has_side_effects=True, vmem_limit_bytes=54 * 2**20
        ),
    )(x, vn, ve, vu)


def solution(mesh):
    counts = {axis: mesh.shape[axis] for axis in ("py", "px", "pz")}
    spec = P(("site", "py"), "px", "pz", None)
    return jax.shard_map(
        functools.partial(body, counts), mesh=mesh, in_specs=(spec,) * 4, out_specs=spec,
        check_vma=False,
    )
```

time: 104 us -> 100 us (0.962)
  local copies, waits for them, and re-layouts: 4.64 us -> 2.02 us
    unnamed x1, local copies, waits for them, and re-layouts: 4.64 us -> 2.02 us
where the time goes in v2:
time: 100 us
  Pallas kernels  98.1 us (98%)
  local copies, waits for them, and re-layouts  2.02 us (2%)
    pallas_call x1, Pallas kernels, body(): pl.pallas_call(functools.partial(kernel, counts, chunks), out_shape=pltpu...  98.1 us
    unnamed x1, local copies, waits for them, and re-layouts  2.02 us

profile of v2, /device:TPU:0, one launch (start us, length us, event | category | flops | bytes accessed | tf_op | source)
XLA Modules:
  0.0 100.1 jit_solution(16345723225349634787)
XLA Ops:
  0.0 98.1 %shard_map.46 = f32[4,64,32,128]{3,2,1,0:T(8,128)S(1)} custom-call(f32[4,64,32,128]{3,2,1,0:T(8,128)} %x.1, f32[4,64,32,128]{3,2,1,0:T(8,128)} %vn.1, f32[4,64,32,128]{3,2,1,0:T(8,128)} %ve.1, f32[4,64,32,128]{3,2,1,0:T(8,128)} %vu.1), custom_call_target="tpu_custom_call" | custom-call | tf_op jit(solution)/shard_map/pallas_call | solution.py:251
  98.1 2.0 %copy.6 = f32[4,64,32,128]{3,2,1,0:T(8,128)} copy(f32[4,64,32,128]{3,2,1,0:T(8,128)S(1)} %shard_map.46) | data formatting | bytes 8388608

commit v3 on v2

v3 whole, which is shorter than its diff:
```python
import functools

import jax
import jax.numpy as jnp
from jax import lax
from jax.experimental import pallas as pl
from jax.experimental.pallas import tpu as pltpu
from jax.sharding import PartitionSpec as P

STEPS = 4
CUTS = ((0, 32, 64), (0, 32, 64), (0, 32, 64), (0, 32, 56, 64))
PAD = 8
MESH = pl.DeviceIdType.MESH


def pieces(rows, t):
    ends = sorted({rows * cut // 64 for cut in CUTS[t]})
    return [(a, b - a) for a, b in zip(ends, ends[1:])]


def kernel(
    counts, x, vn, ve, vu, out, s, w,
    edge_sem, load_sem, speed_sem,
    py_send, py_recv, px_send, px_recv, pz_send, pz_recv,
):
    planes, rows, depth, _ = x.shape
    parts = [pieces(rows, t) for t in range(STEPS)]
    cells = pl.ds(PAD, depth)
    speeds = (vn, ve, vu)
    outer = sorted({1, planes})
    inner_count = planes - 2
    axes = ("py", "px", "pz")
    index = {axis: lax.axis_index(axis) for axis in axes}

    def sends(axis, way):
        return index[axis] < counts[axis] - 1 if way == 0 else index[axis] > 0

    def receives(axis, way):
        return sends(axis, 1 - way)

    def target(axis, way):
        count = counts[axis]
        return {axis: lax.rem(index[axis] + (1 if way == 0 else count - 1), count)}

    def remote(src, dst, send, recv, axis, way):
        return pltpu.make_async_remote_copy(
            src_ref=src, dst_ref=dst, send_sem=send, recv_sem=recv,
            device_id=target(axis, way), device_id_type=MESH,
        )

    def py_copy(way, t, i):
        first, span = parts[t][i]
        here = pl.ds(1 + first, span)
        src = s.at[t, planes if way == 0 else 1, here, cells]
        dst = s.at[t, 0 if way == 0 else planes + 1, here, cells]
        return remote(src, dst, py_send.at[way, t], py_recv.at[way, t, i], "py", way)

    def px_copy(way, t):
        row = rows if way == 0 else 1
        inner = pl.ds(1, planes)
        src = x.at[:, row - 1] if t == 0 else s.at[t, inner, row, cells]
        dst = s.at[t, inner, 0 if way == 0 else rows + 1, cells]
        return remote(src, dst, px_send.at[way, t], px_recv.at[way, t], "px", way)

    def pz_copy(way, t):
        inner, here = pl.ds(1, planes), pl.ds(1, rows)
        first = depth - PAD if way == 0 else 0
        if t == 0:
            src = x.at[:, :, pl.ds(first, PAD)]
        else:
            src = s.at[t, inner, here, pl.ds(PAD + first, PAD)]
        dst = s.at[t, inner, here, pl.ds(0 if way == 0 else PAD + depth, PAD)]
        return remote(src, dst, pz_send.at[way, t], pz_recv.at[way, t], "pz", way)

    def wait_sent(t):
        def py_wait(way):
            block = s.at[t, planes if way == 0 else 1, pl.ds(1, rows), cells]
            remote(block, block, py_send.at[way, t], py_recv.at[way, t, 0], "py", way).wait_send()

        each("py", sends, py_wait)
        each("pz", sends, lambda way: pz_copy(way, t).wait_send())
        each("px", sends, lambda way: px_copy(way, t).wait_send())

    def each(axis, test, action):
        if counts[axis] > 1:
            for way in (0, 1):
                pl.when(test(axis, way))(functools.partial(action, way))

    def send_py(t, i):
        each("py", sends, lambda way: py_copy(way, t, i).start())

    def send_rest(t):
        each("px", sends, lambda way: px_copy(way, t).start())
        each("pz", sends, lambda way: pz_copy(way, t).start())

    def wait_py(t, i):
        each("py", receives, lambda way: py_copy(way, t, i).wait_recv())

    def wait_rest(t):
        each("px", receives, lambda way: px_copy(way, t).wait_recv())
        each("pz", receives, lambda way: pz_copy(way, t).wait_recv())

    def speed_copy(k, i):
        here = pl.ds(*parts[0][i])
        return pltpu.make_async_copy(speeds[k].at[:, here], w.at[k, :, here], speed_sem.at[i])

    def wait_speeds(i):
        block = w.at[:, :, pl.ds(*parts[0][i])]
        pltpu.make_async_copy(block, block, speed_sem.at[i]).wait()

    def edge_load(k, i):
        first, span = parts[0][i]
        return pltpu.make_async_copy(
            x.at[outer[k] - 1, pl.ds(first, span)],
            s.at[0, outer[k], pl.ds(1 + first, span), cells],
            edge_sem.at[k, i],
        )

    for i in range(len(parts[0])):
        for k in range(len(outer)):
            edge_load(k, i).start()
    if inner_count > 0:
        load = pltpu.make_async_copy(
            x.at[pl.ds(1, inner_count)],
            s.at[0, pl.ds(2, inner_count), pl.ds(1, rows), cells],
            load_sem,
        )
        load.start()

    barrier = pltpu.get_barrier_semaphore()
    greeted = 0
    for axis in axes:
        each(axis, sends, lambda way, axis=axis: pl.semaphore_signal(
            barrier, inc=1, device_id=target(axis, way), device_id_type=MESH))
        if counts[axis] > 1:
            for way in (0, 1):
                greeted = greeted + sends(axis, way).astype(jnp.int32)
    pl.semaphore_wait(barrier, greeted)

    for i in range(len(parts[0])):
        for k in range(len(outer)):
            edge_load(k, i).wait()
        send_py(0, i)
    send_rest(0)
    for i in range(len(parts[0])):
        for k in range(3):
            speed_copy(k, i).start()

    def clear(axis, way):
        lanes = s.shape[-1]

        def fill(t, _):
            if axis == "py":
                plane = 0 if way == 0 else planes + 1

                def row_fill(r, _):
                    s[t, plane, 1 + r, PAD:PAD + depth, :] = jnp.zeros((depth, lanes), s.dtype)
                    return None

                lax.fori_loop(0, rows, row_fill, None)
            elif axis == "px":
                row = 0 if way == 0 else rows + 1
                for p in range(1, planes + 1):
                    s[t, p, row, PAD:PAD + depth, :] = jnp.zeros((depth, lanes), s.dtype)
            else:
                first = 0 if way == 0 else PAD + depth

                def row_fill(r, _):
                    for p in range(1, planes + 1):
                        s[t, p, 1 + r, first:first + PAD, :] = jnp.zeros((PAD, lanes), s.dtype)
                    return None

                lax.fori_loop(0, rows, row_fill, None)
            return None

        lax.fori_loop(0, STEPS, fill, None)

    for axis in axes:
        for way in (0, 1):
            pl.when(jnp.logical_not(receives(axis, way)))(functools.partial(clear, axis, way))

    if inner_count > 0:
        load.wait()

    def update(t, piece, wanted):
        def row(r, _):
            for z in range(PAD, PAD + depth, 8):
                here = slice(z, z + 8)
                column = {}
                for p in wanted:
                    for q in (p, p + 1, p + 2):
                        if q not in column:
                            column[q] = s[t, q, r + 1, here, :]
                    lower = (column[p], s[t, p + 1, r, here, :], s[t, p + 1, r + 1, z - 1:z + 7, :])
                    upper = (column[p + 2], s[t, p + 1, r + 2, here, :], s[t, p + 1, r + 1, z + 1:z + 9, :])
                    middle = column[p + 1]
                    value = middle
                    for k in range(3):
                        value = value - w[k, p, r, z - PAD:z - PAD + 8, :] * (upper[k] - lower[k])
                    spread = (lower[0] + upper[0]) + (lower[1] + upper[1]) + (lower[2] + upper[2])
                    value = value + 0.05 * (spread - 6.0 * middle)
                    if t == STEPS - 1:
                        out[p, r, z - PAD:z - PAD + 8, :] = value
                    else:
                        s[t + 1, p + 1, r + 1, here, :] = value
            return None

        lax.fori_loop(piece[0], piece[0] + piece[1], row, None)

    for t in range(STEPS - 1):
        wait_rest(t)
        sent = 0
        for i, piece in enumerate(parts[t]):
            if t == 0:
                wait_speeds(i)
            wait_py(t, i)
            update(t, piece, range(planes))
            while sent < len(parts[t + 1]) and sum(parts[t + 1][sent]) <= sum(piece):
                send_py(t + 1, sent)
                sent += 1
        send_rest(t + 1)

    last = STEPS - 1
    wait_rest(last)
    update(last, (0, rows), range(1, planes - 1))
    for t in range(last):
        wait_sent(t)
    for i, piece in enumerate(parts[last]):
        wait_py(last, i)
        update(last, piece, [p - 1 for p in outer])
    wait_sent(last)


def body(counts, x, vn, ve, vu):
    planes, rows, depth, lanes = x.shape
    most = max(len(pieces(rows, t)) for t in range(STEPS))
    dma = pltpu.SemaphoreType.DMA
    return pl.pallas_call(
        functools.partial(kernel, counts),
        out_shape=pltpu.VMEM(x.shape, x.dtype),
        in_specs=[pl.BlockSpec(memory_space=pl.ANY)] * 4,
        out_specs=pl.BlockSpec(memory_space=pltpu.VMEM),
        scratch_shapes=[
            pltpu.VMEM((STEPS, planes + 2, rows + 2, depth + 2 * PAD, lanes), x.dtype),
            pltpu.VMEM((3, planes, rows, depth, lanes), x.dtype),
            dma((2, most)),
            dma(()),
            dma((most,)),
            dma((2, STEPS)),
            dma((2, STEPS, most)),
            dma((2, STEPS)),
            dma((2, STEPS)),
            dma((2, STEPS)),
            dma((2, STEPS)),
        ],
        compiler_params=pltpu.CompilerParams(
            collective_id=0, has_side_effects=True, vmem_limit_bytes=54 * 2**20
        ),
    )(x, vn, ve, vu)


def solution(mesh):
    counts = {axis: mesh.shape[axis] for axis in ("py", "px", "pz")}
    spec = P(("site", "py"), "px", "pz", None)
    return jax.shard_map(
        functools.partial(body, counts), mesh=mesh, in_specs=(spec,) * 4, out_specs=spec,
        check_vma=False,
    )
```

time: 100 us -> 97.8 us (0.978)
  Pallas kernels: 98.1 us -> 95.7 us
    pallas_call x1, Pallas kernels: 98.1 us -> 95.7 us  [body(): pl.pallas_call(functools.partial(kernel, counts), out_shape=pltpu.VMEM(x....]
where the time goes in v3:
time: 97.8 us; the launch traced here: 97.7 us
  Pallas kernels  95.7 us (98%)
  local copies, waits for them, and re-layouts  2.02 us (2%)
    pallas_call x1, Pallas kernels, body(): pl.pallas_call(functools.partial(kernel, counts), out_shape=pltpu.VMEM(x....  95.7 us
    unnamed x1, local copies, waits for them, and re-layouts  2.02 us

profile of v3, /device:TPU:0, one launch (start us, length us, event | category | flops | bytes accessed | tf_op | source)
XLA Modules:
  0.0 97.7 jit_solution(17477697258464248124)
XLA Ops:
  0.0 95.7 %shard_map.46 = f32[4,64,32,128]{3,2,1,0:T(8,128)S(1)} custom-call(f32[4,64,32,128]{3,2,1,0:T(8,128)} %x.1, f32[4,64,32,128]{3,2,1,0:T(8,128)} %vn.1, f32[4,64,32,128]{3,2,1,0:T(8,128)} %ve.1, f32[4,64,32,128]{3,2,1,0:T(8,128)} %vu.1), custom_call_target="tpu_custom_call" | custom-call | tf_op jit(solution)/shard_map/pallas_call | solution.py:238
  95.7 2.0 %copy.6 = f32[4,64,32,128]{3,2,1,0:T(8,128)} copy(f32[4,64,32,128]{3,2,1,0:T(8,128)S(1)} %shard_map.46) | data formatting | bytes 8388608

commit v4 on v3

--- a/solution.py
+++ b/solution.py
@@ -8,7 +8,7 @@
 from jax.sharding import PartitionSpec as P
 
 STEPS = 4
-CUTS = ((0, 32, 64), (0, 32, 64), (0, 32, 64), (0, 32, 56, 64))
+CUTS = ((0, 32, 64), (0, 32, 64), (0, 32, 64), (0, 32, 56, 62, 64))
 PAD = 8
 MESH = pl.DeviceIdType.MESH
 
@@ -116,6 +116,14 @@
             edge_sem.at[k, i],
         )
 
+    barrier = pltpu.get_barrier_semaphore()
+    greeted = 0
+    for axis in axes:
+        each(axis, sends, lambda way, axis=axis: pl.semaphore_signal(
+            barrier, inc=1, device_id=target(axis, way), device_id_type=MESH))
+        if counts[axis] > 1:
+            for way in (0, 1):
+                greeted = greeted + sends(axis, way).astype(jnp.int32)
     for i in range(len(parts[0])):
         for k in range(len(outer)):
             edge_load(k, i).start()
@@ -127,14 +135,6 @@
         )
         load.start()
 
-    barrier = pltpu.get_barrier_semaphore()
-    greeted = 0
-    for axis in axes:
-        each(axis, sends, lambda way, axis=axis: pl.semaphore_signal(
-            barrier, inc=1, device_id=target(axis, way), device_id_type=MESH))
-        if counts[axis] > 1:
-            for way in (0, 1):
-                greeted = greeted + sends(axis, way).astype(jnp.int32)
     pl.semaphore_wait(barrier, greeted)
 
     for i in range(len(parts[0])):
@@ -223,11 +223,19 @@
     last = STEPS - 1
     wait_rest(last)
     update(last, (0, rows), range(1, planes - 1))
+    split = planes > 1 and counts["py"] > 1
+    if split:
+        for way in (0, 1):
+            pl.when(jnp.logical_not(receives("py", way)))(
+                lambda way=way: update(last, (0, rows), [(planes - 1) * way]))
     for t in range(last):
         wait_sent(t)
     for i, piece in enumerate(parts[last]):
         wait_py(last, i)
-        update(last, piece, [p - 1 for p in outer])
+        if split:
+            each("py", receives, lambda way: update(last, piece, [(planes - 1) * way]))
+        else:
+            update(last, piece, [p - 1 for p in outer])
     wait_sent(last)
 
 

time: 97.8 us -> 97.7 us (level)
  no operation moved by 1% of the time
where the time goes in v4:
time: 97.7 us; the launch traced here: 97.6 us
  Pallas kernels  95.6 us (98%)
  local copies, waits for them, and re-layouts  2.02 us (2%)
    pallas_call x1, Pallas kernels, body(): pl.pallas_call(functools.partial(kernel, counts), out_shape=pltpu.VMEM(x....  95.6 us
    unnamed x1, local copies, waits for them, and re-layouts  2.02 us

profile of v4, /device:TPU:0, one launch (start us, length us, event | category | flops | bytes accessed | tf_op | source)
XLA Modules:
  0.0 97.6 jit_solution(8641882398383730744)
XLA Ops:
  0.0 95.6 %shard_map.46 = f32[4,64,32,128]{3,2,1,0:T(8,128)S(1)} custom-call(f32[4,64,32,128]{3,2,1,0:T(8,128)} %x.1, f32[4,64,32,128]{3,2,1,0:T(8,128)} %vn.1, f32[4,64,32,128]{3,2,1,0:T(8,128)} %ve.1, f32[4,64,32,128]{3,2,1,0:T(8,128)} %vu.1), custom_call_target="tpu_custom_call" | custom-call | tf_op jit(solution)/shard_map/pallas_call | solution.py:246
  95.6 2.0 %copy.6 = f32[4,64,32,128]{3,2,1,0:T(8,128)} copy(f32[4,64,32,128]{3,2,1,0:T(8,128)S(1)} %shard_map.46) | data formatting | bytes 8388608
